TPU v7x, 32 devices: a whole 2x2x4 slice. The times are simulated.
32 devices in a mesh: dp: 2 (over x), expert: 16 (over z, y, core).
Axes of the slice: x: 2, y: 2, z: 4, core: 2. Of those that a mesh axis runs over, the one named last changes fastest.
Arguments:
- cotangent: bfloat16 [4096, 3584], P(('dp', 'expert')), may hold values from -0.59765625 to 0.59765625
- expert_ids: int32 [4096, 1], P(('dp', 'expert')), may hold values from 0 to 3; in each aligned block of 128 rows (0 to 127, 128 to 255, ...) at most 48 rows name the same one
- route_weights: float32 [4096, 1], P(('dp', 'expert')), may hold values from 0.1 to 1
- gate_pre: bfloat16 [1536, 4096], P('dp', 'expert'), may hold values from -5 to 5
- up_pre: bfloat16 [1536, 4096], P('dp', 'expert'), may hold values from -5 to 5
- down_weight: bfloat16 [3584, 4096], P('dp', 'expert'), may hold values from -0.1875 to 0.1875
Outputs:
- weight_grad: bfloat16 [3584, 4096], P('dp', 'expert')
- gate_grad: bfloat16 [1536, 4096], P('dp', 'expert')
- up_grad: bfloat16 [1536, 4096], P('dp', 'expert')
Inputs may be any that keep to these rules, and one draw needn't show every extreme that they name: `expert_ids`: each token names one expert. Among the tokens of one device, at most 48 name the same expert, and in every draw some expert is named by exactly 48 tokens of some device.
All inputs are finite; a program needn't handle non-finite values.
Results may differ from a plain program's by a relative error of at most 0.013.
Values may be sent and summed in bfloat16 or wider, within the bound.
A program may use at most 64 MiB of HBM per device.

v0:
```python
import jax
import jax.numpy as jnp
from jax import lax
from jax.sharding import PartitionSpec as P

SPLIT = 4


def slot_buffer(cotangent, expert_ids, route_weights, experts, capacity):
    columns = lax.broadcasted_iota(jnp.int32, (1, 1, experts), 2)
    onehot = (expert_ids[:, :, None] == columns).astype(jnp.int32)
    touched = jnp.sum(onehot, axis=1)
    earlier = jnp.cumsum(touched, axis=0) - touched
    position = jnp.sum(onehot * earlier[:, None, :], axis=2)
    target = expert_ids * capacity + position
    places = lax.broadcasted_iota(jnp.int32, (1, 1, experts * capacity), 2)
    chosen = (target[:, :, None] == places).astype(jnp.float32)
    picker = jnp.sum(chosen, axis=1)
    slot_scale = jnp.sum(chosen * route_weights[:, :, None], axis=(0, 1))
    picked = lax.dot_general(
        picker.astype(jnp.bfloat16),
        cotangent,
        (((0,), (0,)), ((), ())),
        preferred_element_type=jnp.float32,
    )
    return (picked * slot_scale[:, None]).astype(jnp.bfloat16)


def activations(gate_rows, up_rows, upstream):
    gate_full = gate_rows.astype(jnp.float32)
    up_full = up_rows.astype(jnp.float32)
    sigmoid = jax.nn.sigmoid(gate_full)
    active = gate_full * sigmoid
    product = (active * up_full).astype(jnp.bfloat16)
    gate_grad = (upstream * up_full * sigmoid * (1.0 + gate_full * (1.0 - sigmoid))).astype(
        jnp.bfloat16
    )
    up_grad = (upstream * active).astype(jnp.bfloat16)
    return (product, gate_grad, up_grad)


def per_device(cotangent, expert_ids, route_weights, gate_pre, up_pre, down_weight):
    devices = lax.axis_size("expert")
    experts = devices // SPLIT
    capacity = gate_pre.shape[0] // devices
    width = cotangent.shape[1]
    buffer = slot_buffer(cotangent, expert_ids, route_weights, experts, capacity)
    copies = jnp.broadcast_to(
        buffer.reshape(experts, 1, capacity, width), (experts, SPLIT, capacity, width)
    )
    arrived = lax.all_to_all(
        copies.reshape(devices, capacity, width), "expert", split_axis=0, concat_axis=0, tiled=True
    )
    routed = arrived.reshape(devices * capacity, width)
    columns = routed
    upstream = jnp.dot(
        columns,
        lax.all_gather(down_weight, "dp", axis=0, tiled=True),
        preferred_element_type=jnp.float32,
    )
    product, gate_grad, up_grad = activations(gate_pre, up_pre, upstream)
    columns = routed
    weight_grad = lax.psum_scatter(
        lax.dot_general(
            columns, product, (((0,), (0,)), ((), ())), preferred_element_type=jnp.float32
        ).astype(jnp.bfloat16),
        "dp",
        scatter_dimension=0,
        tiled=True,
    )
    return (weight_grad, gate_grad, up_grad)


def solution(mesh):
    placed = (
        P(("dp", "expert"), None),
        P(("dp", "expert"), None),
        P(("dp", "expert"), None),
        P("dp", "expert"),
        P("dp", "expert"),
        P("dp", "expert"),
    )
    return jax.shard_map(
        per_device,
        mesh=mesh,
        in_specs=placed,
        out_specs=(P("dp", "expert"), P("dp", "expert"), P("dp", "expert")),
        check_vma=False,
    )
```

profile of v0, /device:TPU:0, one launch (start us, length us, event | category | flops | bytes accessed | tf_op | source)
XLA Modules:
  0.0 185.5 jit_solution(10108907824707783767)
XLA Ops:
  7.2 0.0 copy-start
  7.2 3.4 %fusion.16 = s32[128]{0:T(128)S(1)} fusion(s32[128]{0:T(128)} %bitcast.18), kind=kOutput, calls=%fused_computation.30 | output fusion | flops 68480 | bytes 1024 | tf_op jit(solution)/shard_map/jit(cumsum)/reduce_window_sum | solution.py:13
  10.6 0.7 fusion.14
  11.2 0.8 select_reduce_fusion
  12.0 0.0 copy-done
  12.0 0.6 fusion
  12.6 3.0 %broadcast_in_dim.5 = bf16[4,4,48,3584]{3,2,1,0:T(8,128)(2,1)} broadcast(bf16[4,48,3584]{2,1,0:T(8,128)(2,1)S(1)} %bitcast.16), dimensions={0,2,3} | broadcast | bytes 6881280 | tf_op jit(solution)/shard_map/broadcast_in_dim | solution.py:48
  15.6 0.0 copy-start.1
  15.6 0.0 copy-start.2
  15.6 7.6 %all-to-all-start = ((bf16[16,48,3584]{2,1,0:T(8,128)(2,1)}), bf16[16,48,3584]{2,1,0:T(8,128)(2,1)}, u32[]{:S(2)}, u32[]{:S(2)}) async-start(bf16[16,48,3584]{2,1,0:T(8,128)(2,1)} %bitcast.15), calls=%async_computation | async-start | bytes 11010048 | tf_op jit(solution)/shard_map/all_to_all | solution.py:51
  23.2 0.0 all-gather.2.cloned.1.call-start
  23.3 0.7 all-gather.2.cloned.1.call-update
  23.9 0.0 reduce-scatter.2.cloned.1.call-start
  24.0 99.6 %all-to-all-done = bf16[16,48,3584]{2,1,0:T(8,128)(2,1)} async-done(((bf16[16,48,3584]{2,1,0:T(8,128)(2,1)}), bf16[16,48,3584]{2,1,0:T(8,128)(2,1)}, u32[]{:S(2)}, u32[]{:S(2)}) %all-to-all-start) | async-done | bytes 5505056 | tf_op jit(solution)/shard_map/all_to_all | solution.py:51
  123.6 0.0 copy-done.1
  123.6 0.0 copy-done.2
  123.6 5.6 %convolution_convert_fusion = bf16[3584,256]{1,0:T(8,128)(2,1)} fusion(bf16[768,3584]{1,0:T(8,128)(2,1)} %bitcast.6, bf16[768,256]{1,0:T(8,128)(2,1)S(1)} %copy-done.1, bf16[768,256]{1,0:T(8,128)(2,1)S(1)} %copy-done.2), kind=kOutput, calls=%fused_computation.1 | convolution fusion | flops 1411776512 | bytes 8126464 | tf_op jit(solution)/shard_map/dot_general | solution.py:64
  129.2 0.0 reduce-scatter.2.cloned.1.call-update
  129.2 0.0 all-gather.2.cloned.1.call-done
  129.2 5.7 %multiply_convert_fusion = (bf16[768,256]{1,0:T(8,128)(2,1)}, bf16[768,256]{1,0:T(8,128)(2,1)}) fusion(bf16[768,256]{1,0:T(8,128)(2,1)S(1)} %copy-done.2, bf16[768,256]{1,0:T(8,128)(2,1)S(1)} %copy-done.1, bf16[768,3584]{1,0:T(8,128)(2,1)} %bitcast.6, bf16[3584,256]{1,0:T(8,128)(2,1)} %all-gather.2.cloned.1.call-done), kind=kOutput, calls=%fused_computation.16 | convolution fusion | flops 1412235264 | bytes 8912896 | tf_op jit(solution)/shard_map/dot_general | solution.py:56
  135.0 43.7 %reduce-scatter.2.cloned.1.call-done = bf16[1792,256]{1,0:T(8,128)(2,1)} async-done(((bf16[3584,256]{1,0:T(8,128)(2,1)}), bf16[1792,256]{1,0:T(8,128)(2,1)}) %reduce-scatter.2.cloned.1.call-update) | async-done | bytes 917520 | tf_op jit(solution)/shard_map/reduce_scatter | solution.py:63
Async XLA Ops:
  7.2 4.8 %copy-start = (bf16[128,3584]{1,0:T(8,128)(2,1)S(1)}, bf16[128,3584]{1,0:T(8,128)(2,1)}, u32[]{:S(2)}) copy-start(bf16[128,3584]{1,0:T(8,128)(2,1)} %param.6) | copy-start | bytes 2752516
  15.6 108.0 %copy-start.1 = (bf16[768,256]{1,0:T(8,128)(2,1)S(1)}, bf16[768,256]{1,0:T(8,128)(2,1)}, u32[]{:S(2)}) copy-start(bf16[768,256]{1,0:T(8,128)(2,1)} %param.10) | copy-start | bytes 1179652
  15.6 108.0 %copy-start.2 = (bf16[768,256]{1,0:T(8,128)(2,1)S(1)}, bf16[768,256]{1,0:T(8,128)(2,1)}, u32[]{:S(2)}) copy-start(bf16[768,256]{1,0:T(8,128)(2,1)} %param.9) | copy-start | bytes 1179652
  15.6 108.0 %all-to-all-start = ((bf16[16,48,3584]{2,1,0:T(8,128)(2,1)}), bf16[16,48,3584]{2,1,0:T(8,128)(2,1)}, u32[]{:S(2)}, u32[]{:S(2)}) async-start(bf16[16,48,3584]{2,1,0:T(8,128)(2,1)} %bitcast.15), calls=%async_computation | async-start | bytes 11010048 | tf_op jit(solution)/shard_map/all_to_all | solution.py:51
  23.2 106.0 %all-gather.2.cloned.1.call-start = ((), (), s32[]{:S(2)}) async-start(), calls=%async_computation.3 | async-start | bytes 2752512 | tf_op jit(solution)/shard_map/all_gather | solution.py:58
  23.9 154.7 %reduce-scatter.2.cloned.1.call-start = ((), (), s32[]{:S(2)}) async-start(), calls=%async_computation.2 | async-start | bytes 2752512 | tf_op jit(solution)/shard_map/reduce_scatter | solution.py:63
Sparse Core Ops, SparseCore 0:
  25.6 31.4 all-gather.1
  129.3 49.2 reduce-scatter.1
where the time goes:
time: 186 us; the launch traced here: 185 us
  waiting for transfers between devices  144 us (77%)
  between operations  14.1 us (8%)
  matrix products  12 us (6%)
  starting transfers between devices  7.67 us (4%)
  other arithmetic  4.81 us (3%)
  local copies, waits for them, and re-layouts  3 us (2%)
    all_to_all x1, waiting for transfers between devices, per_device(): lax.all_to_all(copies.reshape(devices, capacity, width), 'expert', split_...  99.6 us
    reduce_scatter x1, waiting for transfers between devices, per_device(): lax.psum_scatter(lax.dot_general(columns, product, (((0,), (0,)), ((), ()...  43.7 us
    all_to_all x1, starting transfers between devices, per_device(): lax.all_to_all(copies.reshape(devices, capacity, width), 'expert', split_...  7.59 us
    dot_general x1, matrix products, per_device(): jnp.dot(columns, lax.all_gather(down_weight, 'dp', axis=0, tiled=True), p...  5.74 us
    dot_general x1, matrix products, per_device(): lax.dot_general(columns, product, (((0,), (0,)), ((), ())), preferred_ele...  5.6 us
  transfers between devices with their start and end apart: 3, of which 2 were waited for; matrix products, arithmetic and copies ran while one was open for 6% of the time, Pallas kernels for 0%

commit v1 on v0

v1 whole, which is shorter than its diff:
```python
import functools

import jax
import jax.numpy as jnp
from jax import lax
from jax.experimental import pallas as pl
from jax.experimental.pallas import tpu as pltpu
from jax.sharding import PartitionSpec as P

SPLIT = 4


def kernel(
    sizes,
    cot_ref,
    ids_ref,
    weights_ref,
    gate_ref,
    up_ref,
    down_ref,
    wgrad_ref,
    ggrad_ref,
    ugrad_ref,
    sendbuf,
    routed,
    down_in,
    part_out,
    part_in,
    upstream,
    slope,
    active,
    product,
    picker,
    scale,
    z_send,
    z_recv,
    y_send,
    y_recv,
    c_send,
    c_recv,
    w_send,
    w_recv,
    g_send,
    g_recv,
):
    n, experts, cap, chunks, width, aligned = sizes
    own = chunks // n
    away = chunks - own
    tokens = ids_ref.shape[0]
    dp = lax.axis_index("dp")
    me = lax.axis_index("expert")
    e, lane = me // SPLIT, me % SPLIT
    across = me - lane + (lane + 2) % SPLIT
    beside = me - lane + (lane // 2) * 2 + (lane + 1) % 2
    lane_across = (lane + 2) % SPLIT

    barrier = pltpu.get_barrier_semaphore()

    def greet(target):
        pl.semaphore_signal(
            barrier, inc=1, device_id=target, device_id_type=pl.DeviceIdType.MESH
        )

    for k in range(1, experts):
        greet({"expert": (e + k) % experts * SPLIT + lane})
    greet({"expert": across})
    greet({"expert": beside})
    for k in range(1, n):
        greet({"dp": (dp + k) % n})

    shape = (tokens, tokens)
    first, second = lax.broadcasted_iota(jnp.int32, shape, 0), lax.broadcasted_iota(jnp.int32, shape, 1)
    diagonal = first == second
    ids_row = jnp.sum(jnp.where(diagonal, ids_ref[...], 0), axis=0, keepdims=True)
    weight_row = jnp.sum(jnp.where(diagonal, weights_ref[...], 0.0), axis=0, keepdims=True)
    names = lax.broadcasted_iota(jnp.int32, (-(-experts // 16) * 16, tokens), 0) == ids_row
    before = jnp.where(first < second, 1.0, 0.0).astype(jnp.bfloat16)
    earlier = jnp.dot(
        jnp.where(names, 1.0, 0.0).astype(jnp.bfloat16), before, preferred_element_type=jnp.float32
    )
    position = jnp.sum(jnp.where(names, earlier, 0.0), axis=0, keepdims=True).astype(jnp.int32)
    target = ids_row * cap + position
    chosen = lax.broadcasted_iota(jnp.int32, (experts * cap, tokens), 0) == target
    picker[...] = jnp.where(chosen, 1.0, 0.0).astype(jnp.bfloat16)
    scale[...] = jnp.sum(jnp.where(chosen, weight_row, 0.0), axis=1, keepdims=True)

    def block_of(q):
        return (dp + 1 + q // own) % n * own + q % own

    def build(q):
        if aligned:
            columns = cot_ref[:, pl.ds(pl.multiple_of(block_of(q) * width, 128), width)]
        else:
            columns = cot_ref[block_of(q)]
        picked = jnp.dot(picker[...], columns, preferred_element_type=jnp.float32)
        rows = (picked * scale[...]).astype(jnp.bfloat16).reshape(experts, cap, width)
        sendbuf[q] = rows
        routed[q, e, lane] = sendbuf[q, e]

    def to_expert(q):
        for k in range(1, experts):
            there = (e + k) % experts
            pltpu.make_async_remote_copy(
                src_ref=sendbuf.at[q, there],
                dst_ref=routed.at[q, e, lane],
                send_sem=z_send.at[q],
                recv_sem=z_recv.at[q],
                device_id={"expert": there * SPLIT + lane},
                device_id_type=pl.DeviceIdType.MESH,
            ).start()

    def relay(q, which, to, send, recv):
        return pltpu.make_async_remote_copy(
            src_ref=routed.at[q, :, which],
            dst_ref=routed.at[q, :, which],
            send_sem=send,
            recv_sem=recv,
            device_id={"expert": to},
            device_id_type=pl.DeviceIdType.MESH,
        )

    def over_y(q):
        return relay(q, lane, across, y_send.at[q], y_recv.at[q])

    def over_core(q, turn):
        which = lane if turn == 0 else lane_across
        return relay(q, which, beside, c_send.at[q, turn], c_recv.at[q, turn])

    def down_copy(q):
        piece = q % own
        return pltpu.make_async_remote_copy(
            src_ref=down_ref.at[piece],
            dst_ref=down_in.at[q],
            send_sem=w_send.at[q],
            recv_sem=w_recv.at[q],
            device_id={"dp": (dp - 1 - q // own + n) % n},
            device_id_type=pl.DeviceIdType.MESH,
        )

    def part_copy(q):
        return pltpu.make_async_remote_copy(
            src_ref=part_out.at[q],
            dst_ref=part_in.at[q],
            send_sem=g_send.at[q],
            recv_sem=g_recv.at[q],
            device_id={"dp": (dp + 1 + q // own) % n},
            device_id_type=pl.DeviceIdType.MESH,
        )

    build(0)
    pl.semaphore_wait(barrier, experts - 1 + 2 + n - 1)

    @pl.loop(0, away)
    def _(q):
        down_copy(q).start()

    @pl.loop(1, chunks)
    def _(q):
        build(q)
        to_expert(q - 1)

    to_expert(chunks - 1)

    rows_all = gate_ref.shape[0]
    piece = rows_all // 8

    @pl.loop(0, 8)
    def _(i):
        at = pl.ds(pl.multiple_of(i * piece, 16), piece)
        gate = gate_ref[at, :].astype(jnp.float32)
        up = up_ref[at, :].astype(jnp.float32)
        sig = jax.nn.sigmoid(gate)
        act = gate * sig
        active[at, :] = act
        slope[at, :] = up * sig * (1.0 + gate * (1.0 - sig))
        product[at, :] = (act * up).astype(jnp.bfloat16)
        upstream[at, :] = jnp.zeros_like(act)

    def all_but_one(ref_at, sem):
        pltpu.make_async_copy(ref_at, ref_at, sem).wait()

    def partial_of(q):
        rows = routed[q].reshape(rows_all, width)
        return rows, lax.dot_general(
            rows, product[...], (((0,), (0,)), ((), ())), preferred_element_type=jnp.float32
        ).astype(jnp.bfloat16)

    @pl.loop(0, chunks + 2)
    def _(t):
        @pl.when(t < chunks)
        def _():
            all_but_one(routed.at[t, pl.ds(0, experts - 1), 0], z_recv.at[t])
            over_y(t).start()
            over_core(t, 0).start()

        @pl.when((t >= 1) & (t < chunks + 1))
        def _():
            over_y(t - 1).wait_recv()
            over_core(t - 1, 1).start()

        @pl.when(t >= 2)
        def _():
            q = t - 2
            over_core(q, 0).wait_recv()
            over_core(q, 1).wait_recv()

            @pl.when(q < away)
            def _():
                rows, part = partial_of(q)
                part_out[q] = part
                down_copy(q).wait_recv()
                upstream[...] += jnp.dot(rows, down_in[q], preferred_element_type=jnp.float32)
                part_copy(q).start()

            @pl.when(q >= away)
            def _():
                j = q - away
                rows, part = partial_of(q)
                upstream[...] += jnp.dot(rows, down_ref[j], preferred_element_type=jnp.float32)
                total = part.astype(jnp.float32)
                for k in range(n - 1):
                    part_copy(k * own + j).wait_recv()
                    total = total + part_in[k * own + j].astype(jnp.float32)
                wgrad_ref[j] = total.astype(jnp.bfloat16)

    @pl.loop(0, 8)
    def _(i):
        at = pl.ds(pl.multiple_of(i * piece, 16), piece)
        ggrad_ref[at, :] = (upstream[at, :] * slope[at, :]).astype(jnp.bfloat16)
        ugrad_ref[at, :] = (upstream[at, :] * active[at, :]).astype(jnp.bfloat16)

    @pl.loop(0, chunks)
    def _(q):
        all_but_one(sendbuf.at[q, pl.ds(0, experts - 1)], z_send.at[q])
        over_y(q).wait_send()
        over_core(q, 0).wait_send()
        over_core(q, 1).wait_send()

    @pl.loop(0, away)
    def _(q):
        down_copy(q).wait_send()
        part_copy(q).wait_send()


def chunk_width(depth):
    for width in (256, 128):
        if depth % width == 0:
            return width, True
    return depth, False


def per_device(cotangent, expert_ids, route_weights, gate_pre, up_pre, down_weight):
    n = lax.axis_size("dp")
    devices = lax.axis_size("expert")
    experts = devices // SPLIT
    rows, hidden = gate_pre.shape
    capacity = rows // devices
    cap = -(-capacity // 16) * 16
    depth = down_weight.shape[0]
    width, aligned = chunk_width(depth)
    own = depth // width
    chunks = n * own
    away = chunks - own
    if not aligned:
        cotangent = cotangent.reshape(-1, chunks, width).swapaxes(0, 1)

    def widen(a):
        if cap == capacity:
            return a
        a = a.reshape(devices, capacity, hidden)
        return jnp.pad(a, ((0, 0), (0, cap - capacity), (0, 0))).reshape(devices * cap, hidden)

    def narrow(a):
        if cap == capacity:
            return a
        return a.reshape(devices, cap, hidden)[:, :capacity].reshape(rows, hidden)

    padded = devices * cap
    half, full = jnp.bfloat16, jnp.float32
    vmem = pl.BlockSpec(memory_space=pltpu.VMEM)
    dma = pltpu.SemaphoreType.DMA
    weight_grad, gate_grad, up_grad = pl.pallas_call(
        functools.partial(kernel, (n, experts, cap, chunks, width, aligned)),
        out_shape=(
            jax.ShapeDtypeStruct((own, width, hidden), half),
            jax.ShapeDtypeStruct((padded, hidden), half),
            jax.ShapeDtypeStruct((padded, hidden), half),
        ),
        in_specs=[vmem] * 6,
        out_specs=(vmem, vmem, vmem),
        scratch_shapes=[
            pltpu.VMEM((chunks, experts, cap, width), half),
            pltpu.VMEM((chunks, experts, SPLIT, cap, width), half),
            pltpu.VMEM((away, width, hidden), half),
            pltpu.VMEM((away, width, hidden), half),
            pltpu.VMEM((away, width, hidden), half),
            pltpu.VMEM((padded, hidden), full),
            pltpu.VMEM((padded, hidden), full),
            pltpu.VMEM((padded, hidden), full),
            pltpu.VMEM((padded, hidden), half),
            pltpu.VMEM((experts * cap, cotangent.shape[0] if aligned else cotangent.shape[1]), half),
            pltpu.VMEM((experts * cap, 1), full),
            dma((chunks,)),
            dma((chunks,)),
            dma((chunks,)),
            dma((chunks,)),
            dma((chunks, 2)),
            dma((chunks, 2)),
            dma((away,)),
            dma((away,)),
            dma((away,)),
            dma((away,)),
        ],
        compiler_params=pltpu.CompilerParams(collective_id=0, has_side_effects=True),
    )(
        cotangent,
        expert_ids,
        route_weights,
        widen(gate_pre),
        widen(up_pre),
        down_weight.reshape(own, width, hidden),
    )
    return weight_grad.reshape(depth, hidden), narrow(gate_grad), narrow(up_grad)


def solution(mesh):
    placed = (
        P(("dp", "expert"), None),
        P(("dp", "expert"), None),
        P(("dp", "expert"), None),
        P("dp", "expert"),
        P("dp", "expert"),
        P("dp", "expert"),
    )
    return jax.shard_map(
        per_device,
        mesh=mesh,
        in_specs=placed,
        out_specs=(P("dp", "expert"), P("dp", "expert"), P("dp", "expert")),
        check_vma=False,
    )
```

time: 186 us -> 61.2 us (0.33)
  waiting for transfers between devices: 144 us -> 0 us
  Pallas kernels: 0 us -> 53.8 us
  between operations: 14.1 us -> 0.66 us
  matrix products: 12 us -> 0 us
  starting transfers between devices: 7.67 us -> 0 us
  other arithmetic: 4.81 us -> 0 us
  local copies, waits for them, and re-layouts: 3 us -> 6.23 us
    all_to_all x1 -> x0, waiting for transfers between devices: 99.6 us -> none  [per_device(): lax.all_to_all(copies.reshape(devices, capacity, width), 'expert', split_...]
    pallas_call x0 -> x1, Pallas kernels: none -> 53.8 us  [per_device(): pl.pallas_call(functools.partial(kernel, (n, experts, cap, chunks, width,...]
    reduce_scatter x1 -> x0, waiting for transfers between devices: 43.7 us -> none  [per_device(): lax.psum_scatter(lax.dot_general(columns, product, (((0,), (0,)), ((), ()...]
    dot_general x3 -> x0, matrix products: 12 us -> none  [the longest x1 5.74 us: per_device(): jnp.dot(columns, lax.all_gather(down_weight, 'dp', axis=0, tiled=True), p...]
    all_to_all x1 -> x0, starting transfers between devices: 7.59 us -> none  [per_device(): lax.all_to_all(copies.reshape(devices, capacity, width), 'expert', split_...]
    unnamed x6 -> x13, local copies, waits for them, and re-layouts: 0.02 us -> 6.23 us
    another operation x1 -> x0, other arithmetic: 3.38 us -> none  [slot_buffer(): earlier = jnp.cumsum(touched, axis=0) - touched]
    broadcast_in_dim x1 -> x0, local copies, waits for them, and re-layouts: 2.99 us -> none  [per_device(): jnp.broadcast_to(buffer.reshape(experts, 1, capacity, width), (experts, S...]
  transfers between devices with their start and end apart: 3 -> 0, of which waited for: 2 -> 0; matrix products, arithmetic and copies ran while one was open for 6% -> 0% of each run, Pallas kernels for 0% -> 0%
where the time goes in v1:
time: 61.2 us; the launch traced here: 60.7 us
  Pallas kernels  53.8 us (88%)
  local copies, waits for them, and re-layouts  6.23 us (10%)
  between operations  0.66 us (1%)
    pallas_call x1, Pallas kernels, per_device(): pl.pallas_call(functools.partial(kernel, (n, experts, cap, chunks, width,...  53.8 us
    unnamed x13, local copies, waits for them, and re-layouts  6.23 us

profile of v1, /device:TPU:0, one launch (start us, length us, event | category | flops | bytes accessed | tf_op | source)
XLA Modules:
  0.0 60.7 jit_solution(2433962687356538876)
XLA Ops:
  0.6 0.0 copy-start.2
  0.6 0.6 %copy-done.2 = s32[128,1]{0,1:T(1,128)S(1)} copy-done((s32[128,1]{0,1:T(1,128)S(1)}, s32[128,1]{0,1:T(1,128)}, u32[]{:S(2)}) %copy-start.2) | copy-done | bytes 536
  1.3 0.0 copy-start.3
  1.3 0.7 %copy.9.ids_ref = s32[128,1]{1,0:T(8,128)} copy(s32[128,1]{0,1:T(1,128)S(1)} %copy-done.2) | data formatting | bytes 1024 | tf_op args[1]
  2.0 0.0 copy-done.3
  2.0 0.7 %copy.10.weights_ref = f32[128,1]{1,0:T(8,128)} copy(f32[128,1]{0,1:T(1,128)S(1)} %copy-done.3) | data formatting | bytes 1024 | tf_op args[2]
  2.8 53.8 %shard_map.85 = (bf16[7,256,256]{2,1,0:T(8,128)(2,1)}, bf16[768,256]{1,0:T(8,128)(2,1)}, bf16[768,256]{1,0:T(8,128)(2,1)}) custom-call(bf16[128,3584]{1,0:T(8,128)(2,1)} %cot_ref.1, s32[128,1]{1,0:T(8,128)} %copy.9.ids_ref, f32[128,1]{1,0:T(8,128)} %copy.10.weights_ref, bf16[768,256]{1,0:T(8,128)(2,1)} %gate_ref.1, bf16[768,256]{1,0:T(8,128)(2,1)} %up_ref.1, ...), custom_call_target="tpu_custom_call" | custom-call | tf_op jit(solution)/shard_map/pallas_call | solution.py:282
  56.6 0.0 copy-start.1
  56.6 2.2 %copy.14 = bf16[1792,256]{1,0:T(8,128)(2,1)} copy(bf16[1792,256]{1,0:T(8,128)(2,1)} %bitcast.2) | data formatting | bytes 1835008
  58.8 0.0 copy-done.1
  58.8 0.0 copy-start
  58.8 0.7 %copy.15 = bf16[768,256]{1,0:T(8,128)(2,1)} copy(bf16[768,256]{1,0:T(8,128)(2,1)S(1)} %copy-done.1) | data formatting | bytes 786432
  59.5 0.4 copy-done
  59.9 0.7 %copy.16 = bf16[768,256]{1,0:T(8,128)(2,1)} copy(bf16[768,256]{1,0:T(8,128)(2,1)S(1)} %copy-done) | data formatting | bytes 786432
Async XLA Ops:
  0.6 0.7 %copy-start.2 = (s32[128,1]{0,1:T(1,128)S(1)}, s32[128,1]{0,1:T(1,128)}, u32[]{:S(2)}) copy-start(s32[128,1]{0,1:T(1,128)} %param.7) | copy-start | bytes 1540
  1.3 0.7 %copy-start.3 = (f32[128,1]{0,1:T(1,128)S(1)}, f32[128,1]{0,1:T(1,128)}, u32[]{:S(2)}) copy-start(f32[128,1]{0,1:T(1,128)} %param.8) | copy-start | bytes 1540
  56.6 2.2 %copy-start.1 = (bf16[768,256]{1,0:T(8,128)(2,1)S(1)}, bf16[768,256]{1,0:T(8,128)(2,1)}, u32[]{:S(2)}) copy-start(bf16[768,256]{1,0:T(8,128)(2,1)} %get-tuple-element.13) | copy-start | bytes 1179652
  58.8 1.1 %copy-start = (bf16[768,256]{1,0:T(8,128)(2,1)S(1)}, bf16[768,256]{1,0:T(8,128)(2,1)}, u32[]{:S(2)}) copy-start(bf16[768,256]{1,0:T(8,128)(2,1)} %get-tuple-element.14) | copy-start | bytes 1179652

commit v2 on v1

v2 whole, which is shorter than its diff:
```python
import functools

import jax
import jax.numpy as jnp
from jax import lax
from jax.experimental import pallas as pl
from jax.experimental.pallas import tpu as pltpu
from jax.sharding import PartitionSpec as P

SPLIT = 4
EARLY = 2
BUILD = 3
LAG = 3


def kernel(
    sizes,
    cot_hbm,
    ids_ref,
    weights_ref,
    gate_hbm,
    up_hbm,
    down_hbm,
    wgrad_ref,
    ggrad_ref,
    ugrad_ref,
    cot_ref,
    gate_ref,
    up_ref,
    down_ref,
    load,
    sendbuf,
    routed,
    cot_in,
    ids_in,
    weights_in,
    up_out,
    up_in,
    upstream,
    slope,
    active,
    product,
    picker,
    scale,
    z_send,
    z_recv,
    y_send,
    y_recv,
    c_send,
    c_recv,
    x_send,
    x_recv,
    i_send,
    i_recv,
    p_send,
    p_recv,
    u_send,
    u_recv,
):
    n, experts, cap, chunks, width, aligned = sizes
    own = chunks // n
    away = chunks - own
    early = min(EARLY, own - 1)
    ahead = min(BUILD, chunks)
    tokens = ids_ref.shape[1]
    dp = lax.axis_index("dp")
    me = lax.axis_index("expert")
    e, lane = me // SPLIT, me % SPLIT
    across = me - lane + (lane + 2) % SPLIT
    beside = me - lane + (lane // 2) * 2 + (lane + 1) % 2
    lane_across = (lane + 2) % SPLIT

    loads = [
        pltpu.make_async_copy(source, to, load.at[i])
        for i, (source, to) in enumerate(
            ((cot_hbm, cot_ref), (gate_hbm, gate_ref), (up_hbm, up_ref), (down_hbm, down_ref))
        )
    ]
    for copy in loads:
        copy.start()

    barrier = pltpu.get_barrier_semaphore()

    def greet(target):
        pl.semaphore_signal(
            barrier, inc=1, device_id=target, device_id_type=pl.DeviceIdType.MESH
        )

    for k in range(1, experts):
        greet({"expert": (e + k) % experts * SPLIT + lane})
    greet({"expert": across})
    greet({"expert": beside})
    for k in range(1, n):
        greet({"dp": (dp + k) % n})

    def send(source, to, sent, arrived, device):
        return pltpu.make_async_remote_copy(
            src_ref=source,
            dst_ref=to,
            send_sem=sent,
            recv_sem=arrived,
            device_id=device,
            device_id_type=pl.DeviceIdType.MESH,
        )

    def chunk_at(t):
        late = jnp.where(t < early + away, own - early, -away)
        return t + jnp.where(t < early, 0, late)

    def columns_of(share, j):
        if aligned:
            return cot_ref.at[:, pl.ds(pl.multiple_of((share * own + j) * width, 128), width)]
        return cot_ref.at[share * own + j]

    def cot_copy(i):
        to = (dp - 1 - i // own + n) % n
        return send(columns_of(to, i % own), cot_in.at[i], x_send.at[i], x_recv.at[i], {"dp": to})

    def ids_copy(k):
        return send(
            ids_ref, ids_in.at[k - 1], i_send.at[k - 1, 0], i_recv.at[k - 1, 0], {"dp": (dp - k + n) % n}
        )

    def weights_copy(k):
        return send(
            weights_ref, weights_in.at[k - 1], i_send.at[k - 1, 1], i_recv.at[k - 1, 1], {"dp": (dp - k + n) % n}
        )

    def product_copy(k):
        return send(
            product.at[0], product.at[k], p_send.at[k - 1], p_recv.at[k - 1], {"dp": (dp - k + n) % n}
        )

    def up_copy(i):
        return send(up_out.at[i], up_in.at[i], u_send.at[i], u_recv.at[i], {"dp": (dp + 1 + i) % n})

    def pick(k, ids_row, weight_row):
        shape = (tokens, tokens)
        first = lax.broadcasted_iota(jnp.int32, shape, 0)
        second = lax.broadcasted_iota(jnp.int32, shape, 1)
        names = lax.broadcasted_iota(jnp.int32, (-(-experts // 16) * 16, tokens), 0) == ids_row
        before = jnp.where(first < second, 1.0, 0.0).astype(jnp.bfloat16)
        earlier = jnp.dot(
            jnp.where(names, 1.0, 0.0).astype(jnp.bfloat16), before, preferred_element_type=jnp.float32
        )
        position = jnp.sum(jnp.where(names, earlier, 0.0), axis=0, keepdims=True).astype(jnp.int32)
        target = ids_row * cap + position
        chosen = lax.broadcasted_iota(jnp.int32, (experts * cap, tokens), 0) == target
        picker[k] = jnp.where(chosen, 1.0, 0.0).astype(jnp.bfloat16)
        scale[k] = jnp.sum(jnp.where(chosen, weight_row, 0.0), axis=1, keepdims=True)

    def place(q, k, columns):
        picked = jnp.dot(picker[k], columns, preferred_element_type=jnp.float32)
        rows = (picked * scale[k]).astype(jnp.bfloat16).reshape(experts, cap, width)
        sendbuf[q] = rows
        routed[q, e, lane] = sendbuf[q, e]

    def build(t):
        q = chunk_at(t)

        @pl.when(q < own)
        def _():
            place(q, 0, columns_of(dp, q)[...])

        @pl.when(q >= own)
        def _():
            cot_copy(q - own).wait_recv()
            place(q, q // own, cot_in[q - own])

    def from_source(q, source):
        at = routed.at[q, source, lane]
        return send(at, at, y_send.at[q], y_recv.at[q], {"expert": across})

    def to_expert(t):
        q = chunk_at(t)
        for k in range(1, experts):
            there = (e + k) % experts
            send(
                sendbuf.at[q, there],
                routed.at[q, e, lane],
                z_send.at[q],
                z_recv.at[q],
                {"expert": there * SPLIT + lane},
            ).start()
        from_source(q, e).start()

    def over_y(q):
        at = routed.at[q, :, lane]
        return send(at, at, y_send.at[q], y_recv.at[q], {"expert": across})

    def over_core(q, turn):
        at = routed.at[q, :, lane if turn == 0 else lane_across]
        return send(at, at, c_send.at[q, turn], c_recv.at[q, turn], {"expert": beside})

    def all_but_one(ref_at, sem):
        pltpu.make_async_copy(ref_at, ref_at, sem).wait()

    pick(0, ids_ref[...], weights_ref[...])
    loads[0].wait()
    for j in range(early):
        place(j, 0, columns_of(dp, j)[...])
    pl.semaphore_wait(barrier, experts - 1 + 2 + n - 1)
    for k in range(1, n):
        ids_copy(k).start()
        weights_copy(k).start()

    @pl.loop(0, away)
    def _(i):
        cot_copy(i).start()

    for j in range(early):
        to_expert(j)

    rows_all = gate_ref.shape[0]
    piece = rows_all // 8
    loads[1].wait()
    loads[2].wait()

    @pl.loop(0, 8)
    def _(i):
        at = pl.ds(pl.multiple_of(i * piece, 16), piece)
        gate = gate_ref[at, :].astype(jnp.float32)
        up = up_ref[at, :].astype(jnp.float32)
        sig = jax.nn.sigmoid(gate)
        act = gate * sig
        active[at, :] = act
        slope[at, :] = up * sig * (1.0 + gate * (1.0 - sig))
        product[0, at, :] = (act * up).astype(jnp.bfloat16)
        for k in range(n):
            upstream[k, at, :] = jnp.zeros_like(act)

    for k in range(1, n):
        ids_copy(k).wait_recv()
        weights_copy(k).wait_recv()
        pick(k, ids_in[k - 1], weights_in[k - 1])
    for t in range(early, ahead):
        build(t)
    for t in range(early, ahead - 1):
        to_expert(t)
    for k in range(1, n):
        product_copy(k).start()
    loads[3].wait()

    def gradient(j):
        total = jnp.zeros((width, product.shape[2]), jnp.float32)
        for k in range(n):
            rows = routed[k * own + j].reshape(rows_all, width)
            total = total + lax.dot_general(
                rows, product[k], (((0,), (0,)), ((), ())), preferred_element_type=jnp.float32
            )
        wgrad_ref[j] = total.astype(jnp.bfloat16)

    @pl.loop(0, chunks + LAG + 1)
    def _(t):
        @pl.when(t + ahead < chunks)
        def _():
            build(t + ahead)

        @pl.when(t + ahead - 1 < chunks)
        def _():
            to_expert(t + ahead - 1)

        @pl.when(t < chunks)
        def _():
            q = chunk_at(t)
            all_but_one(routed.at[q, pl.ds(0, experts - 1), 0], z_recv.at[q])
            for k in range(1, experts):
                from_source(q, (e + k) % experts).start()
            over_core(q, 0).start()

        @pl.when((t >= LAG) & (t < chunks + LAG))
        def _():
            q = chunk_at(t - LAG)
            over_y(q).wait_recv()
            over_core(q, 1).start()

        @pl.when(t >= LAG + 1)
        def _():
            turn = t - LAG - 1
            q = chunk_at(turn)
            k, j = q // own, q % own
            over_core(q, 0).wait_recv()
            over_core(q, 1).wait_recv()
            rows = routed[q].reshape(rows_all, width)
            upstream[k] += jnp.dot(rows, down_ref[j], preferred_element_type=jnp.float32)

            @pl.when((k >= 1) & (j == own - 1))
            def _():
                up_out[k - 1] = upstream[k].astype(jnp.bfloat16)

            @pl.when(turn == early + away)
            def _():
                for i in range(1, n):
                    product_copy(i).wait_recv()
                for i in range(early):
                    gradient(i)

            @pl.when(turn >= early + away)
            def _():
                gradient(j)

            @pl.when((k >= 1) & (j == own - 1))
            def _():
                up_copy(k - 1).start()

    for k in range(1, n):
        up_copy(k - 1).wait_recv()

    @pl.loop(0, 8)
    def _(i):
        at = pl.ds(pl.multiple_of(i * piece, 16), piece)
        total = upstream[0, at, :]
        for k in range(1, n):
            total = total + up_in[k - 1, at, :].astype(jnp.float32)
        ggrad_ref[at, :] = (total * slope[at, :]).astype(jnp.bfloat16)
        ugrad_ref[at, :] = (total * active[at, :]).astype(jnp.bfloat16)

    @pl.loop(0, chunks)
    def _(q):
        all_but_one(sendbuf.at[q, pl.ds(0, experts - 1)], z_send.at[q])
        over_y(q).wait_send()
        over_core(q, 0).wait_send()
        over_core(q, 1).wait_send()

    @pl.loop(0, away)
    def _(i):
        cot_copy(i).wait_send()

    for k in range(1, n):
        ids_copy(k).wait_send()
        weights_copy(k).wait_send()
        product_copy(k).wait_send()
        up_copy(k - 1).wait_send()


def chunk_width(depth):
    for width in (256, 128):
        if depth % width == 0:
            return width, True
    return depth, False


def per_device(cotangent, expert_ids, route_weights, gate_pre, up_pre, down_weight):
    n = lax.axis_size("dp")
    devices = lax.axis_size("expert")
    experts = devices // SPLIT
    rows, hidden = gate_pre.shape
    capacity = rows // devices
    cap = -(-capacity // 16) * 16
    depth = down_weight.shape[0]
    width, aligned = chunk_width(depth)
    own = depth // width
    chunks = n * own
    away = chunks - own
    if not aligned:
        cotangent = cotangent.reshape(-1, chunks, width).swapaxes(0, 1)

    def widen(a):
        if cap == capacity:
            return a
        a = a.reshape(devices, capacity, hidden)
        return jnp.pad(a, ((0, 0), (0, cap - capacity), (0, 0))).reshape(devices * cap, hidden)

    def narrow(a):
        if cap == capacity:
            return a
        return a.reshape(devices, cap, hidden)[:, :capacity].reshape(rows, hidden)

    padded = devices * cap
    tokens = expert_ids.shape[0]
    half, full = jnp.bfloat16, jnp.float32
    vmem = pl.BlockSpec(memory_space=pltpu.VMEM)
    anywhere = pl.BlockSpec(memory_space=pl.ANY)
    dma = pltpu.SemaphoreType.DMA
    weight_grad, gate_grad, up_grad = pl.pallas_call(
        functools.partial(kernel, (n, experts, cap, chunks, width, aligned)),
        out_shape=(
            jax.ShapeDtypeStruct((own, width, hidden), half),
            jax.ShapeDtypeStruct((padded, hidden), half),
            jax.ShapeDtypeStruct((padded, hidden), half),
        ),
        in_specs=[anywhere, vmem, vmem, anywhere, anywhere, anywhere],
        out_specs=(vmem, vmem, vmem),
        scratch_shapes=[
            pltpu.VMEM(cotangent.shape, half),
            pltpu.VMEM((padded, hidden), half),
            pltpu.VMEM((padded, hidden), half),
            pltpu.VMEM((own, width, hidden), half),
            dma((4,)),
            pltpu.VMEM((chunks, experts, cap, width), half),
            pltpu.VMEM((chunks, experts, SPLIT, cap, width), half),
            pltpu.VMEM((away, tokens, width), half),
            pltpu.VMEM((n - 1, 1, tokens), jnp.int32),
            pltpu.VMEM((n - 1, 1, tokens), full),
            pltpu.VMEM((n - 1, padded, hidden), half),
            pltpu.VMEM((n - 1, padded, hidden), half),
            pltpu.VMEM((n, padded, hidden), full),
            pltpu.VMEM((padded, hidden), full),
            pltpu.VMEM((padded, hidden), full),
            pltpu.VMEM((n, padded, hidden), half),
            pltpu.VMEM((n, experts * cap, tokens), half),
            pltpu.VMEM((n, experts * cap, 1), full),
            dma((chunks,)),
            dma((chunks,)),
            dma((chunks,)),
            dma((chunks,)),
            dma((chunks, 2)),
            dma((chunks, 2)),
            dma((away,)),
            dma((away,)),
            dma((n - 1, 2)),
            dma((n - 1, 2)),
            dma((n - 1,)),
            dma((n - 1,)),
            dma((n - 1,)),
            dma((n - 1,)),
        ],
        compiler_params=pltpu.CompilerParams(collective_id=0, has_side_effects=True),
    )(
        cotangent,
        expert_ids.reshape(1, -1),
        route_weights.reshape(1, -1),
        widen(gate_pre),
        widen(up_pre),
        down_weight.reshape(own, width, hidden),
    )
    return weight_grad.reshape(depth, hidden), narrow(gate_grad), narrow(up_grad)


def solution(mesh):
    placed = (
        P(("dp", "expert"), None),
        P(("dp", "expert"), None),
        P(("dp", "expert"), None),
        P("dp", "expert"),
        P("dp", "expert"),
        P("dp", "expert"),
    )
    return jax.shard_map(
        per_device,
        mesh=mesh,
        in_specs=placed,
        out_specs=(P("dp", "expert"), P("dp", "expert"), P("dp", "expert")),
        check_vma=False,
    )
```

time: 61.2 us -> 53.3 us (0.87)
  Pallas kernels: 53.8 us -> 48.3 us
  local copies, waits for them, and re-layouts: 6.23 us -> 4.1 us
    pallas_call x1, Pallas kernels: 53.8 us -> 48.3 us  [per_device(): pl.pallas_call(functools.partial(kernel, (n, experts, cap, chunks, width,...]
    unnamed x13 -> x7, local copies, waits for them, and re-layouts: 6.23 us -> 4.1 us
where the time goes in v2:
time: 53.3 us; the launch traced here: 53.1 us
  Pallas kernels  48.3 us (91%)
  local copies, waits for them, and re-layouts  4.1 us (8%)
  between operations  0.65 us (1%)
    pallas_call x1, Pallas kernels, per_device(): pl.pallas_call(functools.partial(kernel, (n, experts, cap, chunks, width,...  48.3 us
    unnamed x7, local copies, waits for them, and re-layouts  4.1 us

profile of v2, /device:TPU:0, one launch (start us, length us, event | category | flops | bytes accessed | tf_op | source)
XLA Modules:
  0.0 53.1 jit_solution(15257021217683323537)
XLA Ops:
  0.6 48.3 %shard_map.85 = (bf16[7,256,256]{2,1,0:T(8,128)(2,1)}, bf16[768,256]{1,0:T(8,128)(2,1)}, bf16[768,256]{1,0:T(8,128)(2,1)}) custom-call(bf16[128,3584]{1,0:T(8,128)(2,1)} %cot_hbm.1, s32[1,128]{1,0:T(1,128)} %bitcast.6, f32[1,128]{1,0:T(1,128)} %bitcast.7, bf16[768,256]{1,0:T(8,128)(2,1)} %gate_hbm.1, bf16[768,256]{1,0:T(8,128)(2,1)} %up_hbm.1, ...), custom_call_target="tpu_custom_call" | custom-call | tf_op jit(solution)/shard_map/pallas_call | solution.py:375
  49.0 0.0 copy-start.1
  49.0 2.2 %copy.12 = bf16[1792,256]{1,0:T(8,128)(2,1)} copy(bf16[1792,256]{1,0:T(8,128)(2,1)} %bitcast.4) | data formatting | bytes 1835008
  51.2 0.0 copy-done.1
  51.2 0.0 copy-start
  51.2 0.7 %copy.13 = bf16[768,256]{1,0:T(8,128)(2,1)} copy(bf16[768,256]{1,0:T(8,128)(2,1)S(1)} %copy-done.1) | data formatting | bytes 786432
  51.9 0.4 copy-done
  52.3 0.7 %copy.14 = bf16[768,256]{1,0:T(8,128)(2,1)} copy(bf16[768,256]{1,0:T(8,128)(2,1)S(1)} %copy-done) | data formatting | bytes 786432
Async XLA Ops:
  49.0 2.2 %copy-start.1 = (bf16[768,256]{1,0:T(8,128)(2,1)S(1)}, bf16[768,256]{1,0:T(8,128)(2,1)}, u32[]{:S(2)}) copy-start(bf16[768,256]{1,0:T(8,128)(2,1)} %get-tuple-element.13) | copy-start | bytes 1179652
  51.2 1.1 %copy-start = (bf16[768,256]{1,0:T(8,128)(2,1)S(1)}, bf16[768,256]{1,0:T(8,128)(2,1)}, u32[]{:S(2)}) copy-start(bf16[768,256]{1,0:T(8,128)(2,1)} %get-tuple-element.14) | copy-start | bytes 1179652

commit v3 on v2

--- a/solution.py
+++ b/solution.py
@@ -16,8 +16,8 @@
 def kernel(
     sizes,
     cot_hbm,
-    ids_ref,
-    weights_ref,
+    ids_hbm,
+    weights_hbm,
     gate_hbm,
     up_hbm,
     down_hbm,
@@ -25,6 +25,8 @@
     ggrad_ref,
     ugrad_ref,
     cot_ref,
+    ids_ref,
+    weights_ref,
     gate_ref,
     up_ref,
     down_ref,
@@ -73,11 +75,18 @@
     loads = [
         pltpu.make_async_copy(source, to, load.at[i])
         for i, (source, to) in enumerate(
-            ((cot_hbm, cot_ref), (gate_hbm, gate_ref), (up_hbm, up_ref), (down_hbm, down_ref))
+            (
+                (cot_hbm, cot_ref),
+                (gate_hbm, gate_ref),
+                (up_hbm, up_ref),
+                (down_hbm, down_ref),
+                (ids_hbm, ids_ref),
+                (weights_hbm, weights_ref),
+            )
         )
     ]
-    for copy in loads:
-        copy.start()
+    for i in (4, 5, 0, 1, 2, 3):
+        loads[i].start()
 
     barrier = pltpu.get_barrier_semaphore()
 
@@ -195,6 +204,8 @@
     def all_but_one(ref_at, sem):
         pltpu.make_async_copy(ref_at, ref_at, sem).wait()
 
+    loads[4].wait()
+    loads[5].wait()
     pick(0, ids_ref[...], weights_ref[...])
     loads[0].wait()
     for j in range(early):
@@ -370,23 +381,25 @@
     tokens = expert_ids.shape[0]
     half, full = jnp.bfloat16, jnp.float32
     vmem = pl.BlockSpec(memory_space=pltpu.VMEM)
-    anywhere = pl.BlockSpec(memory_space=pl.ANY)
+    anywhere = pl.BlockSpec(memory_space=pltpu.HBM)
     dma = pltpu.SemaphoreType.DMA
     weight_grad, gate_grad, up_grad = pl.pallas_call(
         functools.partial(kernel, (n, experts, cap, chunks, width, aligned)),
         out_shape=(
-            jax.ShapeDtypeStruct((own, width, hidden), half),
-            jax.ShapeDtypeStruct((padded, hidden), half),
-            jax.ShapeDtypeStruct((padded, hidden), half),
+            pltpu.VMEM((own, width, hidden), half),
+            pltpu.VMEM((padded, hidden), half),
+            pltpu.VMEM((padded, hidden), half),
         ),
-        in_specs=[anywhere, vmem, vmem, anywhere, anywhere, anywhere],
+        in_specs=[anywhere] * 6,
         out_specs=(vmem, vmem, vmem),
         scratch_shapes=[
             pltpu.VMEM(cotangent.shape, half),
+            pltpu.VMEM((1, tokens), jnp.int32),
+            pltpu.VMEM((1, tokens), full),
             pltpu.VMEM((padded, hidden), half),
             pltpu.VMEM((padded, hidden), half),
             pltpu.VMEM((own, width, hidden), half),
-            dma((4,)),
+            dma((6,)),
             pltpu.VMEM((chunks, experts, cap, width), half),
             pltpu.VMEM((chunks, experts, SPLIT, cap, width), half),
             pltpu.VMEM((away, tokens, width), half),

time: 53.3 us -> 49.7 us (0.932)
  Pallas kernels: 48.3 us -> 46.5 us
  local copies, waits for them, and re-layouts: 4.1 us -> 2.42 us
    pallas_call x1, Pallas kernels: 48.3 us -> 46.5 us  [per_device(): pl.pallas_call(functools.partial(kernel, (n, experts, cap, chunks, width,...]
    unnamed x7 -> x3, local copies, waits for them, and re-layouts: 4.1 us -> 2.42 us
where the time goes in v3:
time: 49.7 us; the launch traced here: 49.6 us
  Pallas kernels  46.5 us (94%)
  local copies, waits for them, and re-layouts  2.42 us (5%)
  between operations  0.64 us (1%)
    pallas_call x1, Pallas kernels, per_device(): pl.pallas_call(functools.partial(kernel, (n, experts, cap, chunks, width,...  46.5 us
    unnamed x3, local copies, waits for them, and re-layouts  2.42 us

profile of v3, /device:TPU:0, one launch (start us, length us, event | category | flops | bytes accessed | tf_op | source)
XLA Modules:
  0.0 49.6 jit_solution(13098162660621652923)
XLA Ops:
  0.6 46.5 %shard_map.85 = (bf16[7,256,256]{2,1,0:T(8,128)(2,1)S(1)}, bf16[768,256]{1,0:T(8,128)(2,1)S(1)}, bf16[768,256]{1,0:T(8,128)(2,1)S(1)}) custom-call(bf16[128,3584]{1,0:T(8,128)(2,1)} %cot_hbm.1, s32[1,128]{1,0:T(1,128)} %bitcast.6, f32[1,128]{1,0:T(1,128)} %bitcast.7, bf16[768,256]{1,0:T(8,128)(2,1)} %gate_hbm.1, bf16[768,256]{1,0:T(8,128)(2,1)} %up_hbm.1, ...), custom_call_target="tpu_custom_call" | custom-call | tf_op jit(solution)/shard_map/pallas_call | solution.py:386
  47.2 0.9 %copy.12 = bf16[1792,256]{1,0:T(8,128)(2,1)} copy(bf16[1792,256]{1,0:T(8,128)(2,1)S(1)} %bitcast.4) | data formatting | bytes 1835008
  48.1 0.7 %copy.13 = bf16[768,256]{1,0:T(8,128)(2,1)} copy(bf16[768,256]{1,0:T(8,128)(2,1)S(1)} %get-tuple-element.10) | data formatting | bytes 786432
  48.8 0.7 %copy.14 = bf16[768,256]{1,0:T(8,128)(2,1)} copy(bf16[768,256]{1,0:T(8,128)(2,1)S(1)} %get-tuple-element.11) | data formatting | bytes 786432

commit v4 on v3

--- a/solution.py
+++ b/solution.py
@@ -10,7 +10,7 @@
 SPLIT = 4
 EARLY = 2
 BUILD = 3
-LAG = 3
+LAG = 2
 
 
 def kernel(

time: 49.7 us -> 48.2 us (0.970)
  Pallas kernels: 46.5 us -> 45 us
    pallas_call x1, Pallas kernels: 46.5 us -> 45 us  [per_device(): pl.pallas_call(functools.partial(kernel, (n, experts, cap, chunks, width,...]
where the time goes in v4:
time: 48.2 us; the launch traced here: 48 us
  Pallas kernels  45 us (93%)
  local copies, waits for them, and re-layouts  2.42 us (5%)
  between operations  0.64 us (1%)
    pallas_call x1, Pallas kernels, per_device(): pl.pallas_call(functools.partial(kernel, (n, experts, cap, chunks, width,...  45 us
    unnamed x3, local copies, waits for them, and re-layouts  2.42 us

profile of v4, /device:TPU:0, one launch (start us, length us, event | category | flops | bytes accessed | tf_op | source)
XLA Modules:
  0.0 48.0 jit_solution(4148448631675846605)
XLA Ops:
  0.6 45.0 %shard_map.85 = (bf16[7,256,256]{2,1,0:T(8,128)(2,1)S(1)}, bf16[768,256]{1,0:T(8,128)(2,1)S(1)}, bf16[768,256]{1,0:T(8,128)(2,1)S(1)}) custom-call(bf16[128,3584]{1,0:T(8,128)(2,1)} %cot_hbm.1, s32[1,128]{1,0:T(1,128)} %bitcast.6, f32[1,128]{1,0:T(1,128)} %bitcast.7, bf16[768,256]{1,0:T(8,128)(2,1)} %gate_hbm.1, bf16[768,256]{1,0:T(8,128)(2,1)} %up_hbm.1, ...), custom_call_target="tpu_custom_call" | custom-call | tf_op jit(solution)/shard_map/pallas_call | solution.py:386
  45.6 0.9 %copy.12 = bf16[1792,256]{1,0:T(8,128)(2,1)} copy(bf16[1792,256]{1,0:T(8,128)(2,1)S(1)} %bitcast.4) | data formatting | bytes 1835008
  46.5 0.7 %copy.13 = bf16[768,256]{1,0:T(8,128)(2,1)} copy(bf16[768,256]{1,0:T(8,128)(2,1)S(1)} %get-tuple-element.10) | data formatting | bytes 786432
  47.3 0.7 %copy.14 = bf16[768,256]{1,0:T(8,128)(2,1)} copy(bf16[768,256]{1,0:T(8,128)(2,1)S(1)} %get-tuple-element.11) | data formatting | bytes 786432
